TPU v7x, 32 devices: a whole 2x2x4 slice. The times are simulated.
32 devices in a mesh: freq: 8 (over z, y), rows: 4 (over x, core).
Axes of the slice: x: 2, y: 2, z: 4, core: 2. Of those that a mesh axis runs over, the one named last changes fastest.
Arguments:
- wavefield: bfloat16 [10240, 32, 1024], P('freq', 'rows'), may hold values from -6 to 6
- u_factors: bfloat16 [2, 16, 4, 256, 512], P(None, 'freq', 'rows'), may hold values from -0.25 to 0.25
- v_factors: bfloat16 [2, 16, 4, 512, 256], P(None, 'freq', 'rows'), may hold values from -0.375 to 0.375
- tile_ranks: int32 [16, 4, 40], P('freq', 'rows'), may hold values from 1 to 64, as said below
- tile_offsets: int32 [16, 4, 40], P('freq', 'rows'), may hold values from 0 to 511, as said below
Outputs:
- convolved: bfloat16 [1024, 32, 1024], P(('rows', 'freq'))
Inputs may be any that keep to these rules, and one draw needn't show every extreme that they name: tile_ranks[k, i, j] is the rank of tile (i, j) of frequency k; the ranks of one tile row sum to at most 512, exactly 512 on some row of every draw, and every tile row has a tile of rank 64. tile_offsets[k, i, j] is the sum of tile_ranks[k, i, j2] over j2 < j.
All inputs are finite; a program needn't handle non-finite values.
Results may differ from a plain program's by a relative error of at most 0.0072.
Values may be sent and summed in bfloat16 or wider, within the bound.
No kernel may reach another device: no remote copies, remote signals or barrier semaphores. Data moves between devices by JAX's collectives and lax.ppermute only.
A program may use at most 128 MiB of HBM per device.

v0:
```python
import functools
import math

import jax
import jax.numpy as jnp
from jax import lax
from jax.sharding import PartitionSpec as P

RANK_MAX = 64


def spectral_tables(freq_count, sample_count):
    freq_bins = jnp.arange(freq_count, dtype=jnp.int32) + 1
    sample_index = jnp.arange(sample_count, dtype=jnp.int32)
    phase_int = freq_bins[:, None] * sample_index[None, :] % sample_count
    angles = phase_int.astype(jnp.float32) * (2.0 * math.pi / sample_count)
    cosine = jnp.cos(angles)
    minus_sine = -jnp.sin(angles)
    stacked = jnp.stack([cosine, minus_sine], axis=1)
    forward = (stacked / math.sqrt(sample_count)).astype(jnp.bfloat16)
    inverse = (stacked / math.sqrt(freq_count)).astype(jnp.bfloat16)
    return (forward, inverse)


def tile_windows(v_row, u_row, starts, rank_max):
    columns = starts.shape[0]
    slot_index = (starts[:, None] + jnp.arange(rank_max, dtype=jnp.int32)[None, :]).reshape(-1)
    v_padded = jnp.pad(v_row, ((0, 0), (0, rank_max), (0, 0)))
    u_padded = jnp.pad(u_row, ((0, 0), (0, 0), (0, rank_max)))
    v_win = jnp.take(v_padded, slot_index, axis=1).reshape(2, columns, rank_max, v_row.shape[2])
    u_win = jnp.take(u_padded, slot_index, axis=2).reshape(2, u_row.shape[1], columns, rank_max)
    return (v_win, u_win)


def slot_lookup(starts, counts, rank_max, slot_count):
    position = jnp.arange(slot_count, dtype=jnp.int32)
    started = starts[:, None, :] <= position[None, :, None]
    owner_tile = jnp.sum(started.astype(jnp.int32), axis=2) - 1
    first_slot = jnp.max(jnp.where(started, starts[:, None, :], 0), axis=2)
    within = position[None, :] - first_slot
    live_slot = position[None, :] < (starts[:, -1] + counts[:, -1])[:, None]
    flat_index = jnp.where(live_slot, owner_tile * rank_max + within, 0)
    return (flat_index, live_slot)


def take_slots(values, chosen):
    return jnp.take(values, chosen, axis=1)


def per_device(wavefield, u_factors, v_factors, tile_ranks, tile_offsets):
    rec_dev, src_dev, samples = wavefield.shape
    freq_dev = u_factors.shape[1]
    rows_dev = u_factors.shape[2]
    tile_size = u_factors.shape[3]
    slot_count = u_factors.shape[4]
    freq_group = lax.axis_size("freq")
    row_group = lax.axis_size("rows")
    freqs = freq_dev * freq_group
    receivers = rec_dev * freq_group
    columns = receivers // tile_size
    sources = src_dev * row_group
    forward, inverse = spectral_tables(freqs, samples)
    spectrum = jnp.einsum("kct,rst->kcrs", forward, wavefield, preferred_element_type=jnp.float32)
    spectrum = spectrum.astype(jnp.bfloat16).reshape(freqs, 2, rec_dev * src_dev)
    windows = jax.vmap(
        functools.partial(tile_windows, rank_max=RANK_MAX), in_axes=(1, 1, 0), out_axes=(1, 1)
    )
    rank_slots = jnp.arange(RANK_MAX, dtype=jnp.int32)
    tile_row = 0
    v_win, u_win = windows(
        v_factors[:, :, tile_row], u_factors[:, :, tile_row], tile_offsets[:, tile_row]
    )
    rank_mask = rank_slots[None, None, :] < tile_ranks[:, tile_row, :, None]
    flat_index, live_slot = slot_lookup(
        tile_offsets[:, tile_row], tile_ranks[:, tile_row], RANK_MAX, slot_count
    )
    prepared = [(v_win, u_win, rank_mask, flat_index, live_slot)]
    by_frequency = lax.all_to_all(spectrum, "freq", split_axis=0, concat_axis=2, tiled=True)
    portion = lax.all_gather(by_frequency[None], "rows", axis=0, tiled=True)
    blocks_in = portion.shape[0]
    spectra = portion.reshape(blocks_in, freq_dev, 2, columns, tile_size, src_dev)
    spectra = jnp.transpose(spectra, (1, 2, 3, 4, 0, 5)).reshape(
        freq_dev, 2, columns, tile_size, blocks_in * src_dev
    )
    tile_row = 0
    v_win, u_win, rank_mask, flat_index, live_slot = prepared[tile_row]
    quadrants = jnp.einsum(
        "afjmr,fbjrs->fabjms", v_win, spectra, preferred_element_type=jnp.float32
    )
    coeffs = jnp.stack(
        [quadrants[:, 0, 0] - quadrants[:, 1, 1], quadrants[:, 0, 1] + quadrants[:, 1, 0]], axis=1
    )
    coeffs = jnp.where(rank_mask[:, None, :, :, None], coeffs, 0.0).astype(jnp.bfloat16)
    stacked = coeffs.reshape(freq_dev, 2, columns * RANK_MAX, blocks_in * src_dev)
    packed = jax.vmap(take_slots)(stacked, flat_index)
    packed = jnp.where(live_slot[:, None, :, None], packed, jnp.zeros((), jnp.bfloat16))
    products = jnp.einsum(
        "afrk,fcks->facrs", u_factors[:, :, tile_row], packed, preferred_element_type=jnp.float32
    )
    results = [
        jnp.stack(
            [products[:, 0, 0] - products[:, 1, 1], products[:, 0, 1] + products[:, 1, 0]], axis=1
        )
    ]
    merged = jnp.stack(results, axis=2)
    bands = merged.astype(jnp.bfloat16).reshape(
        freq_dev, 2, rows_dev * tile_size, blocks_in, src_dev
    )
    bands = bands.reshape(freq_dev, 2, rows_dev * tile_size * sources)
    returned = lax.all_to_all(bands, "freq", split_axis=2, concat_axis=0, tiled=True)
    series = jnp.einsum("kcq,kct->qt", returned, inverse, preferred_element_type=jnp.float32)
    return series.astype(jnp.bfloat16).reshape(rows_dev * tile_size // freq_group, sources, samples)


def solution(mesh):
    placed = (
        P("freq", "rows", None),
        P(None, "freq", "rows", None, None),
        P(None, "freq", "rows", None, None),
        P("freq", "rows", None),
        P("freq", "rows", None),
    )
    return jax.shard_map(
        per_device,
        mesh=mesh,
        in_specs=placed,
        out_specs=P(("rows", "freq"), None, None),
        check_vma=False,
    )
```

profile of v0, /device:TPU:0, one launch (start us, length us, event | category | flops | bytes accessed | tf_op | source)
XLA Modules:
  0.0 294.8 jit_solution(15557455718139508555)
XLA Ops:
  6.5 0.3 fusion.33
  6.9 24.3 %fusion.6 = bf16[16,2,1280,8]{2,0,3,1:T(8,128)(2,1)S(1)} fusion(bf16[1280,8,1024]{2,1,0:T(8,128)(2,1)} %param.5, f32[16,1,1024]{2,0,1:T(8,128)S(1)} %get-tuple-element.14, f32[16,1,1024]{2,0,1:T(8,128)S(1)} %get-tuple-element.13), kind=kOutput, calls=%fused_computation.10 | convolution fusion | flops 671514624 | bytes 21757952 | tf_op jit(solution)/shard_map/kct,rst->kcrs/dot_general | solution.py:63
  31.2 4.5 %copy.92 = bf16[16,2,1280,8]{0,3,2,1:T(8,128)(2,1)} copy(bf16[16,2,1280,8]{2,0,3,1:T(8,128)(2,1)S(1)} %fusion.6) | data formatting | bytes 1310720 | tf_op jit(solution)/shard_map/convert_element_type | solution.py:64
  35.7 4.8 %copy.93 = bf16[16,2,10240]{2,1,0:T(2,128)(2,1)S(1)} copy(bf16[16,2,10240]{0,2,1:T(8,128)(2,1)} %bitcast.107) | data formatting | bytes 1310720 | tf_op jit(solution)/shard_map/reshape | solution.py:64
  40.5 24.9 %all_to_all.33 = bf16[16,2,10240]{2,1,0:T(2,128)(2,1)S(1)} all-to-all(bf16[16,2,10240]{2,1,0:T(2,128)(2,1)S(1)} %copy.93), channel_id=1, replica_groups=mesh['freq'=8,'rows'=4] {'freq'}, dimensions={0} | all-to-all | bytes 1310720 | tf_op jit(solution)/shard_map/all_to_all | solution.py:78
  65.5 0.4 copy.94
  65.8 1.2 broadcast_in_dim.78
  67.4 1.1 copy.141
  68.5 1.0 pad_bitcast_fusion
  69.5 45.7 %gather_fusion = bf16[5120,2,256]{2,1,0:T(2,128)(2,1)} fusion(bf16[2,2,576,256]{3,1,2,0:T(2,128)(2,1)S(1)} %pad_bitcast_fusion, s32[5120]{0:T(1024)S(1)} %reshape.407), kind=kCustom, calls=%fused_computation | custom fusion | bytes 10526720 | tf_op jit(solution)/shard_map/vmap(jit(_take))/gather | solution.py:30
  115.2 5.5 %copy.97 = bf16[2,2560,2,256]{3,1,2,0:T(8,128)(2,1)} copy(bf16[2,2560,2,256]{3,2,1,0:T(2,128)(2,1)} %bitcast.106) | data formatting | bytes 10485760 | tf_op jit(solution)/shard_map/vmap(jit(_take))/gather | solution.py:30
  120.9 0.2 add_reduce_fusion
  121.5 74.5 %reshape.404 = bf16[4,2,2,40,256,8]{5,4,3,2,1,0:T(8,128)(2,1)} reshape(bf16[4,2,2,81920]{3,2,1,0:T(2,128)(2,1)} %all-gather.2.cloned.1.call-done) | data formatting | bytes 5242880 | tf_op jit(solution)/shard_map/reshape | solution.py:81
  196.0 30.3 %copy.95 = bf16[2,2,40,256,4,8]{3,5,4,1,2,0:T(8,128)(2,1)} copy(bf16[2,2,40,256,4,8]{5,3,2,1,0,4:T(8,128)(2,1)} %bitcast.104) | data formatting | bytes 5242880 | tf_op jit(solution)/shard_map/transpose | solution.py:82
  226.3 5.3 %fusion.9 = f32[2,2,2,40,64,32]{4,5,1,2,3,0:T(8,128)S(1)} fusion(bf16[2,2,40,256,4,8]{3,5,4,1,2,0:T(8,128)(2,1)} %copy.95, bf16[2,2,40,64,256]{4,3,2,1,0:T(8,128)(2,1)} %bitcast.110, pred[2,40,64]{2,1,0:T(8,128)(4,1)S(1)} %fusion.32), kind=kOutput, calls=%fused_computation.11 | convolution fusion | flops 338165760 | bytes 10490880 | tf_op jit(solution)/shard_map/afjmr,fbjrs->fabjms/dot_general | solution.py:87
  231.6 0.6 slice_subtract_fusion
  232.2 0.3 copy.99
  232.5 0.4 sub.52
  232.9 0.3 copy.100
  233.2 0.4 add.171
  233.7 4.1 %copy.103 = bf16[2,2,2560,32]{3,1,2,0:T(2,128)(2,1)} copy(bf16[2,2,2560,32]{2,3,1,0:T(8,128)(2,1)S(1)} %fusion.14) | data formatting | bytes 1310720 | tf_op jit(solution)/shard_map/convert_element_type | solution.py:93
  237.7 6.2 %gather_fusion.1 = bf16[1024,2,32]{2,1,0:T(2,128)(2,1)S(1)} fusion(bf16[2,2,2560,32]{3,1,2,0:T(2,128)(2,1)} %copy.103, s32[1024]{0:T(1024)S(1)} %bitcast.105), kind=kCustom, calls=%fused_computation.1 | custom fusion | bytes 270336 | tf_op jit(solution)/shard_map/vmap(jit(_take))/gather | solution.py:47
  244.0 0.4 copy.119
  244.5 0.4 convolution_bitcast_fusion
  245.1 0.2 add.176
  245.4 0.2 sub.55
  245.7 6.9 %copy.109 = bf16[2,2,8192]{0,1,2:T(2,128)(2,1)} copy(bf16[2,2,8192]{2,0,1:T(2,128)(2,1)S(1)} %pad_maximum_fusion.1) | data formatting | bytes 131072 | tf_op jit(solution)/shard_map/stack | solution.py:101
  252.6 7.2 %reshape.427 = bf16[8,2,2048]{2,1,0:T(2,128)(2,1)S(1)} reshape(bf16[8192,2,2]{2,1,0:T(2,128)(2,1)} %bitcast.108) | data formatting | bytes 131072
  259.7 10.0 %all_to_all.34 = bf16[8,2,2048]{2,1,0:T(2,128)(2,1)S(1)} all-to-all(bf16[8,2,2048]{2,1,0:T(2,128)(2,1)S(1)} %reshape.427), channel_id=1, replica_groups=mesh['freq'=8,'rows'=4] {'freq'}, dimensions={0} | all-to-all | bytes 131072 | tf_op jit(solution)/shard_map/all_to_all | solution.py:110
  269.7 10.0 %reshape.428 = bf16[8192,2,2]{2,1,0:T(2,128)(2,1)} reshape(bf16[8,2,2048]{2,1,0:T(2,128)(2,1)S(1)} %all_to_all.34) | data formatting | bytes 131072
  279.7 6.1 %copy.124 = bf16[2,2,8,1024]{3,2,1,0:T(8,128)(2,1)S(1)} copy(bf16[2,2,8,1024]{0,1,3,2:T(2,128)(2,1)} %bitcast.109) | data formatting | bytes 131072 | tf_op jit(solution)/shard_map/all_to_all | solution.py:110
  285.9 2.1 bitcast_convert_fusion
  (34 shorter events, 1.6 us)
Async XLA Ops:
  6.5 238.0 %copy-start = (bf16[2,2,1,256,512]{4,3,2,1,0:T(8,128)(2,1)S(1)}, bf16[2,2,1,256,512]{4,3,2,1,0:T(8,128)(2,1)}, u32[]{:S(2)}) copy-start(bf16[2,2,1,256,512]{4,3,2,1,0:T(8,128)(2,1)} %param.6) | copy-start | bytes 3145732
  6.5 115.0 %all-gather.2.cloned.1.call-start = ((), (), s32[]{:S(2)}) async-start(), calls=%async_computation.2 | async-start | bytes 3276800 | tf_op jit(solution)/shard_map/all_gather | solution.py:79
  40.5 26.6 %copy-start.2 = (s32[2,1,40]{2,1,0:T(1,128)S(1)}, s32[2,1,40]{2,1,0:T(1,128)}, u32[]{:S(2)}) copy-start(s32[2,1,40]{2,1,0:T(1,128)} %param.9) | copy-start | bytes 964
  40.5 26.9 %copy-start.1 = (bf16[2,2,1,512,256]{4,3,2,1,0:T(8,128)(2,1)S(1)}, bf16[2,2,1,512,256]{4,3,2,1,0:T(8,128)(2,1)}, u32[]{:S(2)}) copy-start(bf16[2,2,1,512,256]{4,3,2,1,0:T(8,128)(2,1)} %param.7) | copy-start | bytes 3145732
  115.2 5.5 %copy-start.3 = (s32[2,1,40]{2,1,0:T(1,128)S(1)}, s32[2,1,40]{2,1,0:T(1,128)}, u32[]{:S(2)}) copy-start(s32[2,1,40]{2,1,0:T(1,128)} %param.8) | copy-start | bytes 964
Sparse Core Ops, SparseCore 0:
  67.2 24.1 all-gather.1
where the time goes:
time: 296 us; the launch traced here: 295 us
  local copies, waits for them, and re-layouts  212 us (72%)
  blocking collectives  34.9 us (12%)
  matrix products  32.1 us (11%)
  between operations  13.7 us (5%)
    reshape x1, local copies, waits for them, and re-layouts, per_device(): portion.reshape(blocks_in, freq_dev, 2, columns, tile_size, src_dev)  74.5 us
    gather x3, local copies, waits for them, and re-layouts, tile_windows(): jnp.take(v_padded, slot_index, axis=1)  51.3 us
    transpose x1, local copies, waits for them, and re-layouts, per_device(): jnp.transpose(spectra, (1, 2, 3, 4, 0, 5))  30.3 us
    all_to_all x1, blocking collectives, per_device(): lax.all_to_all(spectrum, 'freq', split_axis=0, concat_axis=2, tiled=True)  24.9 us
    dot_general x1, matrix products, per_device(): jnp.einsum('kct,rst->kcrs', forward, wavefield, preferred_element_type=jn...  24.3 us
    unnamed x12, local copies, waits for them, and re-layouts  18.3 us
    all_to_all x1, blocking collectives, per_device(): lax.all_to_all(bands, 'freq', split_axis=2, concat_axis=0, tiled=True)  9.97 us
    another operation x1, local copies, waits for them, and re-layouts, per_device(): jnp.stack([products[:, 0, 0] - products[:, 1, 1], products[:, 0, 1] + pro...  6.87 us
  transfers between devices with their start and end apart: 1, of which 0 were waited for; matrix products, arithmetic and copies ran while one was open for 18% of the time, Pallas kernels for 0%

commit v1 on v0

--- a/solution.py
+++ b/solution.py
@@ -4,9 +4,14 @@
 import jax
 import jax.numpy as jnp
 from jax import lax
+from jax.experimental import pallas as pl
+from jax.experimental.pallas import tpu as pltpu
 from jax.sharding import PartitionSpec as P
 
 RANK_MAX = 64
+LANES = 128
+SUBLANES = 8
+NT = (((1,), (1,)), ((), ()))
 
 
 def spectral_tables(freq_count, sample_count):
@@ -112,6 +117,274 @@
     return series.astype(jnp.bfloat16).reshape(rows_dev * tile_size // freq_group, sources, samples)
 
 
+def transform_kernel(traces_ref, table_ref, out_ref, rows_ref, turned_ref):
+    rows, kinds = rows_ref.shape[0], out_ref.shape[0] * out_ref.shape[1] // SUBLANES
+    rows_ref[...] = jnp.dot(traces_ref[...], table_ref[...], preferred_element_type=jnp.float32)
+    for source in range(SUBLANES):
+        part = rows_ref[pl.ds(source, rows // SUBLANES, stride=SUBLANES), :]
+        turned_ref[pl.ds(source, kinds, stride=SUBLANES), :] = part.T[:kinds]
+    out_ref[...] = turned_ref[...].astype(jnp.bfloat16).reshape(out_ref.shape)
+
+
+def transform(traces, table, groups):
+    rows, samples = traces.shape
+    receivers = rows // SUBLANES
+    kinds = table.shape[1]
+    padded = jnp.pad(table, ((0, 0), (0, LANES - kinds)))
+    block = LANES
+    return pl.pallas_call(
+        transform_kernel,
+        grid=(receivers // block,),
+        in_specs=[
+            pl.BlockSpec((block * SUBLANES, samples), lambda i: (i, 0)),
+            pl.BlockSpec((samples, LANES), lambda i: (0, 0)),
+        ],
+        out_specs=pl.BlockSpec((groups, kinds * SUBLANES // groups, block), lambda i: (0, 0, i)),
+        out_shape=jax.ShapeDtypeStruct(
+            (groups, kinds * SUBLANES // groups, receivers), jnp.bfloat16
+        ),
+        scratch_shapes=[
+            pltpu.VMEM((block * SUBLANES, LANES), jnp.float32),
+            pltpu.VMEM((kinds * SUBLANES, block), jnp.float32),
+        ],
+        cost_estimate=pl.CostEstimate(
+            flops=2 * rows * samples * LANES, bytes_accessed=rows * samples * 2, transcendentals=0
+        ),
+        name="transform",
+    )(traces, padded)
+
+
+def coefficient_kernel(
+    place_ref, offsets_ref, totals_ref, own_ref, twin_ref, v_ref, v_far_ref, out_ref, far_ref, lhs_ref
+):
+    groups, rows, receivers = own_ref.shape
+    tile = v_ref.shape[3]
+    freqs = v_ref.shape[1]
+    slots = v_ref.shape[2]
+    per_group = receivers // tile
+    columns = groups * per_group
+    core = place_ref[0]
+    half = 2 * SUBLANES
+    for k in range(freqs):
+        for ref, at in ((own_ref, core), (twin_ref, 1 - core)):
+            for column in range(columns):
+                group, inner = divmod(column, per_group)
+                start = pl.multiple_of(column * 2 * half + at * half, half)
+                lhs_ref[k, pl.ds(start, half), :] = ref[
+                    group, k * half : (k + 1) * half, inner * tile : (inner + 1) * tile
+                ]
+    for side, (v, out) in enumerate(((v_ref, out_ref), (v_far_ref, far_ref))):
+        for k in range(freqs):
+            for low in range(0, slots, tile):
+                slot = lax.broadcasted_iota(jnp.int32, (2 * half, tile), 1) + low
+                chosen = []
+                for part in range(2):
+                    products = lax.dot_general(
+                        lhs_ref[k],
+                        v[part, k, low : low + tile, :],
+                        NT,
+                        preferred_element_type=jnp.float32,
+                    )
+                    value = products[: 2 * half]
+                    for column in range(1, columns):
+                        value = jnp.where(
+                            slot >= offsets_ref[side, k, column],
+                            products[column * 2 * half : (column + 1) * 2 * half],
+                            value,
+                        )
+                    chosen.append(jnp.where(slot < totals_ref[side, k], value, 0.0))
+                by_real, by_imag = chosen
+                n = SUBLANES
+                real = [by_real[g : g + n] - by_imag[g + n : g + 2 * n] for g in (0, half)]
+                imag = [by_real[g + n : g + 2 * n] + by_imag[g : g + n] for g in (0, half)]
+                out[k, 0, :, low : low + tile] = jnp.concatenate(real, 0).astype(jnp.bfloat16)
+                out[k, 1, :, low : low + tile] = jnp.concatenate(imag, 0).astype(jnp.bfloat16)
+
+
+def coefficients(place, offsets, totals, own, twin, v_own, v_far):
+    freqs, slots = v_own.shape[1], v_own.shape[2]
+    tile = v_own.shape[3]
+    columns = own.shape[0] * own.shape[2] // tile
+    smem = pl.BlockSpec(memory_space=pltpu.SMEM)
+    vmem = pl.BlockSpec(memory_space=pltpu.VMEM)
+    shape = jax.ShapeDtypeStruct((freqs, 2, 2 * SUBLANES, slots), jnp.bfloat16)
+    return pl.pallas_call(
+        coefficient_kernel,
+        in_specs=[smem] * 3 + [vmem] * 4,
+        out_specs=[vmem] * 2,
+        out_shape=[shape, shape],
+        scratch_shapes=[pltpu.VMEM((freqs, columns * 4 * SUBLANES, tile), jnp.bfloat16)],
+        cost_estimate=pl.CostEstimate(
+            flops=2 * 4 * freqs * slots * columns * 4 * SUBLANES * tile,
+            bytes_accessed=4 * 2**20,
+            transcendentals=0,
+        ),
+        name="coefficients",
+    )(place, offsets, totals, own, twin, v_own, v_far)
+
+
+def band_kernel(place_ref, near_ref, far_ref, u_ref, out_ref, rhs_ref, turned_ref, bands_ref, mix_ref):
+    freqs, _, sources, slots = near_ref.shape
+    tile = u_ref.shape[2]
+    groups = out_ref.shape[0]
+    place = place_ref[1]
+    wide = 2 * sources
+    rhs_ref[...] = jnp.zeros_like(rhs_ref)
+    turned_ref[...] = jnp.zeros_like(turned_ref)
+    for k in range(freqs):
+        for part in range(2):
+            for ref, at in ((near_ref, place), (far_ref, 1 - place)):
+                value = ref[k, part]
+                start = (2 * k + part) * wide + at * sources
+                rhs_ref[k, pl.ds(pl.multiple_of(start, sources), sources), :] = value
+                start = (2 * k + 1 - part) * wide + at * sources
+                turned_ref[k, pl.ds(pl.multiple_of(start, sources), sources), :] = (
+                    value if part == 0 else -value
+                )
+    total = jnp.zeros((tile, 2 * freqs * wide), jnp.float32)
+    for k in range(freqs):
+        for part, ref in enumerate((rhs_ref, turned_ref)):
+            total += lax.dot_general(u_ref[part, k], ref[k], NT, preferred_element_type=jnp.float32)
+    bands_ref[...] = total
+    packs = LANES // wide
+    kinds = 2 * freqs
+    block = lax.broadcasted_iota(jnp.int32, (tile // packs, LANES), 1) // wide
+    loaded = [bands_ref[pl.ds(b, tile // packs, stride=packs), :] for b in range(packs)]
+    rows = tile // packs // groups
+    for kind in range(kinds):
+        mixed = jnp.zeros((tile // packs, LANES), jnp.float32)
+        for b in range(packs):
+            shift = (b - kind) * wide % LANES
+            moved = pltpu.roll(loaded[b], shift, 1) if shift else loaded[b]
+            mixed = jnp.where(block == b, moved, mixed)
+        mix_ref[:, kind * rows : (kind + 1) * rows, :] = mixed.reshape(groups, rows, LANES)
+    out_ref[...] = mix_ref[...].astype(jnp.bfloat16)
+
+
+def bands_of(place, near, far, u_own, groups):
+    freqs, _, sources, slots = near.shape
+    tile = u_own.shape[2]
+    kinds = 2 * freqs
+    smem = pl.BlockSpec(memory_space=pltpu.SMEM)
+    vmem = pl.BlockSpec(memory_space=pltpu.VMEM)
+    rows = kinds * tile * 2 * sources // LANES // groups
+    return pl.pallas_call(
+        band_kernel,
+        in_specs=[smem] + [vmem] * 3,
+        out_specs=vmem,
+        out_shape=jax.ShapeDtypeStruct((groups, rows, LANES), jnp.bfloat16),
+        scratch_shapes=[
+            pltpu.VMEM((freqs, LANES, slots), jnp.bfloat16),
+            pltpu.VMEM((freqs, LANES, slots), jnp.bfloat16),
+            pltpu.VMEM((tile, LANES), jnp.float32),
+            pltpu.VMEM((groups, rows, LANES), jnp.float32),
+        ],
+        cost_estimate=pl.CostEstimate(
+            flops=2 * 2 * freqs * tile * LANES * slots, bytes_accessed=2**21, transcendentals=0
+        ),
+        name="bands",
+    )(place, near, far, u_own)
+
+
+def series_kernel(bands_ref, inverse_ref, out_ref, wide_ref):
+    groups, rows, lanes = bands_ref.shape
+    kinds = inverse_ref.shape[0]
+    step = groups * rows // kinds
+
+    @pl.when(pl.program_id(0) == 0)
+    def _():
+        wide_ref[...] = bands_ref[...].astype(jnp.float32).reshape(groups * rows, lanes)
+
+    part = wide_ref[pl.ds(pl.program_id(0), kinds, stride=step), :]
+    out_ref[...] = jnp.dot(
+        part.T.astype(jnp.bfloat16), inverse_ref[...], preferred_element_type=jnp.float32
+    ).astype(jnp.bfloat16)
+
+
+def series_of(bands, inverse):
+    groups, rows, lanes = bands.shape
+    kinds, samples = inverse.shape
+    step = groups * rows // kinds
+    return pl.pallas_call(
+        series_kernel,
+        grid=(step,),
+        in_specs=[
+            pl.BlockSpec(bands.shape, lambda i: (0, 0, 0)),
+            pl.BlockSpec(inverse.shape, lambda i: (0, 0)),
+        ],
+        out_specs=pl.BlockSpec((lanes, samples), lambda i: (i, 0)),
+        out_shape=jax.ShapeDtypeStruct((step * lanes, samples), jnp.bfloat16),
+        scratch_shapes=[pltpu.VMEM((groups * rows, lanes), jnp.float32)],
+        cost_estimate=pl.CostEstimate(
+            flops=2 * step * lanes * kinds * samples,
+            bytes_accessed=step * lanes * samples * 2,
+            transcendentals=0,
+        ),
+        name="series",
+    )(bands, inverse)
+
+
+def fits(rec_dev, src_dev, freq_dev, rows_dev, tile, slots, freq_group, row_group):
+    kinds = 2 * freq_dev * freq_group
+    return (
+        src_dev == SUBLANES
+        and row_group == 4
+        and rows_dev == 1
+        and rec_dev % tile == 0
+        and tile % (4 * LANES // 2) == 0
+        and slots % tile == 0
+        and kinds <= LANES
+        and 2 * freq_dev * src_dev * row_group == LANES
+        and tile % (4 * SUBLANES * freq_group) == 0
+    )
+
+
+def per_device_fast(wavefield, u_factors, v_factors, tile_ranks, tile_offsets):
+    rec_dev, src_dev, samples = wavefield.shape
+    freq_dev = u_factors.shape[1]
+    freq_group = lax.axis_size("freq")
+    row_group = lax.axis_size("rows")
+    freqs = freq_dev * freq_group
+    sources = src_dev * row_group
+    tile = u_factors.shape[3]
+    row = lax.axis_index("rows")
+    place = jnp.stack([row % 2, row // 2]).astype(jnp.int32)
+    across = [(i, i ^ 2) for i in range(row_group)]
+    beside = [(i, i ^ 1) for i in range(row_group)]
+    forward, inverse = spectral_tables(freqs, samples)
+    u_own, v_own = u_factors[:, :, 0], v_factors[:, :, 0]
+    v_far = lax.ppermute(v_own, "rows", across)
+    offsets = tile_offsets[:, 0]
+    ends = (offsets[:, -1] + tile_ranks[:, 0, -1])[:, None]
+    lookup = jnp.concatenate([offsets, ends], axis=1)
+    lookup = jnp.stack([lookup, lax.ppermute(lookup, "rows", across)])
+    table = forward.reshape(2 * freqs, samples).T
+    spectrum = transform(wavefield.reshape(rec_dev * src_dev, samples), table, freq_group)
+    own = lax.all_to_all(spectrum, "freq", split_axis=0, concat_axis=0, tiled=True)
+    twin = lax.ppermute(own, "rows", beside)
+    near, leaving = coefficients(place, lookup, lookup[:, :, -1], own, twin, v_own, v_far)
+    far = lax.ppermute(leaving, "rows", across)
+    bands = bands_of(place, near, far, u_own, freq_group)
+    returned = lax.all_to_all(bands, "freq", split_axis=0, concat_axis=0, tiled=True)
+    series = series_of(returned, inverse.reshape(2 * freqs, samples))
+    return series.reshape(tile // freq_group, sources, samples)
+
+
+def choose(wavefield, u_factors, v_factors, tile_ranks, tile_offsets):
+    ok = fits(
+        wavefield.shape[0],
+        wavefield.shape[1],
+        u_factors.shape[1],
+        u_factors.shape[2],
+        u_factors.shape[3],
+        u_factors.shape[4],
+        lax.axis_size("freq"),
+        lax.axis_size("rows"),
+    )
+    step = per_device_fast if ok else per_device
+    return step(wavefield, u_factors, v_factors, tile_ranks, tile_offsets)
+
+
 def solution(mesh):
     placed = (
         P("freq", "rows", None),
@@ -121,7 +394,7 @@
         P("freq", "rows", None),
     )
     return jax.shard_map(
-        per_device,
+        choose,
         mesh=mesh,
         in_specs=placed,
         out_specs=P(("rows", "freq"), None, None),

time: 296 us -> 83.4 us (0.28)
  local copies, waits for them, and re-layouts: 212 us -> 4.89 us
  blocking collectives: 34.9 us -> 0 us
  matrix products: 32.1 us -> 0 us
  waiting for transfers between devices: 0.04 us -> 30 us
  Pallas kernels: 0 us -> 27.9 us
  starting transfers between devices: 0.01 us -> 17.5 us
  between operations: 13.7 us -> 0.07 us
    reshape x2 -> x0, local copies, waits for them, and re-layouts: 79.3 us -> none  [the longest x1 74.5 us: per_device(): portion.reshape(blocks_in, freq_dev, 2, columns, tile_size, src_dev)]
    gather x5 -> x0, local copies, waits for them, and re-layouts: 57.9 us -> none  [the longest x3 51.3 us: tile_windows(): jnp.take(v_padded, slot_index, axis=1)]
    all_to_all x2 -> x0, blocking collectives: 34.9 us -> none  [the longest x1 24.9 us: per_device(): lax.all_to_all(spectrum, 'freq', split_axis=0, concat_axis=2, tiled=True)]
    dot_general x4 -> x0, matrix products: 32.1 us -> none  [the longest x1 24.3 us: per_device(): jnp.einsum('kct,rst->kcrs', forward, wavefield, preferred_element_type=jn...]
    transpose x2 -> x0, local copies, waits for them, and re-layouts: 31.3 us -> none  [the longest x1 30.3 us: per_device(): jnp.transpose(spectra, (1, 2, 3, 4, 0, 5))]
    pallas_call x0 -> x4, Pallas kernels: none -> 27.9 us  [the longest x1 14.7 us: transform(): pl.pallas_call(transform_kernel, grid=(receivers // block,), in_specs=[pl...]
    all_to_all x0 -> x2, waiting for transfers between devices: none -> 21.8 us  [the longest x1 15.7 us: per_device_fast(): lax.all_to_all(spectrum, 'freq', split_axis=0, concat_axis=0, tiled=True)]
    unnamed x12 -> x16, local copies, waits for them, and re-layouts: 18.3 us -> 3.08 us
  transfers between devices with their start and end apart: 1 -> 6, of which waited for: 0 -> 4; matrix products, arithmetic and copies ran while one was open for 18% -> 4% of each run, Pallas kernels for 0% -> 0%
where the time goes in v1:
time: 83.4 us; the launch traced here: 82.9 us
  waiting for transfers between devices  30 us (36%)
  Pallas kernels  27.9 us (33%)
  starting transfers between devices  17.5 us (21%)
  local copies, waits for them, and re-layouts  4.89 us (6%)
  other arithmetic  2.54 us (3%)
    all_to_all x1, waiting for transfers between devices, per_device_fast(): lax.all_to_all(spectrum, 'freq', split_axis=0, concat_axis=0, tiled=True)  15.7 us
    pallas_call x1, Pallas kernels, transform(): pl.pallas_call(transform_kernel, grid=(receivers // block,), in_specs=[pl...  14.7 us
    all_to_all x1, starting transfers between devices, per_device_fast(): lax.all_to_all(spectrum, 'freq', split_axis=0, concat_axis=0, tiled=True)  7.32 us
    all_to_all x1, waiting for transfers between devices, per_device_fast(): lax.all_to_all(bands, 'freq', split_axis=0, concat_axis=0, tiled=True)  6.19 us
    all_to_all x1, starting transfers between devices, per_device_fast(): lax.all_to_all(bands, 'freq', split_axis=0, concat_axis=0, tiled=True)  5.65 us
    pallas_call x1, Pallas kernels, coefficients(): pl.pallas_call(coefficient_kernel, in_specs=[smem] * 3 + [vmem] * 4, out_...  5.58 us
    ppermute x1, waiting for transfers between devices, per_device_fast(): lookup = jnp.stack([lookup, lax.ppermute(lookup, 'rows', across)])  5.16 us
    pallas_call x1, Pallas kernels, series_of(): pl.pallas_call(series_kernel, grid=(step,), in_specs=[pl.BlockSpec(bands....  5.06 us
  transfers between devices with their start and end apart: 6, of which 4 were waited for; matrix products, arithmetic and copies ran while one was open for 4% of the time, Pallas kernels for 0%

profile of v1, /device:TPU:0, one launch (start us, length us, event | category | flops | bytes accessed | tf_op | source)
XLA Modules:
  0.0 82.9 jit_solution(17054141326433239866)
XLA Ops:
  0.0 0.3 fusion.6
  0.4 0.1 copy.11
  0.5 0.2 copy.12
  0.7 0.8 pad.4.table_ref
  1.4 14.7 %transform.1 = bf16[8,32,1280]{2,1,0:T(8,128)(2,1)} custom-call(bf16[10240,1024]{1,0:T(8,128)(2,1)} %bitcast.12, bf16[1024,128]{1,0:T(8,128)(2,1)} %pad.4.table_ref), custom_call_target="tpu_custom_call" | custom-call | flops 2684354560 | bytes 20971520 | tf_op jit(solution)/shard_map/transform/pallas_call | solution.py:135
  16.1 7.3 %all-to-all-start = ((bf16[8,32,1280]{2,1,0:T(8,128)(2,1)}), bf16[8,32,1280]{2,1,0:T(8,128)(2,1)S(1)}, u32[]{:S(2)}, u32[]{:S(2)}) async-start(bf16[8,32,1280]{2,1,0:T(8,128)(2,1)} %transform.1), calls=%async_computation | async-start | bytes 1310720 | tf_op jit(solution)/shard_map/all_to_all | solution.py:363
  23.5 1.5 %collective-permute-start.2 = (bf16[2,2,512,256]{3,2,1,0:T(8,128)(2,1)S(1)}, bf16[2,2,512,256]{3,2,1,0:T(8,128)(2,1)S(1)}, u32[]{:S(2)}, u32[]{:S(2)}) collective-permute-start(bf16[2,2,512,256]{3,2,1,0:T(8,128)(2,1)S(1)} %bitcast.22), channel_id=1, source_target_pairs={{0,2},{1,3},{2,0},{3,1},{4,6},{5,7},{6,4},{7,5},{8,10},{9,11},{10,... | collective-permute-start | bytes 3145736 | tf_op jit(solution)/shard_map/ppermute | solution.py:356
  25.0 0.1 slice.10
  25.1 15.7 %all-to-all-done.own_ref = bf16[8,32,1280]{2,1,0:T(8,128)(2,1)S(1)} async-done(((bf16[8,32,1280]{2,1,0:T(8,128)(2,1)}), bf16[8,32,1280]{2,1,0:T(8,128)(2,1)S(1)}, u32[]{:S(2)}, u32[]{:S(2)}) %all-to-all-start) | async-done | bytes 655392 | tf_op jit(solution)/shard_map/all_to_all | solution.py:363
  40.7 0.0 collective-permute-start.1
  40.8 0.1 slice_add_fusion
  40.8 0.1 pad_add_fusion.1
  40.9 1.5 %collective-permute-start = (s32[2,41]{1,0:T(2,128)S(1)}, s32[2,41]{1,0:T(2,128)S(1)}, u32[]{:S(2)}, u32[]{:S(2)}) collective-permute-start(s32[2,41]{1,0:T(2,128)S(1)} %pad_add_fusion.1), channel_id=1, source_target_pairs={{0,2},{1,3},{2,0},{3,1},{4,6},{5,7},{6,4},{7,5},{8,10},{9,11},{10,... | collective-permute-start | bytes 992 | tf_op jit(solution)/shard_map/ppermute | solution.py:360
  42.4 0.1 fusion.9
  42.5 0.6 pad_add_fusion.2.place_ref
  43.0 5.2 %collective-permute-done = s32[2,41]{1,0:T(2,128)S(1)} collective-permute-done((s32[2,41]{1,0:T(2,128)S(1)}, s32[2,41]{1,0:T(2,128)S(1)}, u32[]{:S(2)}, u32[]{:S(2)}) %collective-permute-start) | collective-permute-done | bytes 360 | tf_op jit(solution)/shard_map/ppermute | solution.py:360
  48.2 0.8 fusion.8.totals_ref
  49.0 0.6 pad_add_fusion.offsets_ref
  49.6 0.0 collective-permute-done.2.v_far_ref
  49.6 1.0 %copy-done.6 = bf16[2,2,512,256]{3,2,1,0:T(8,128)(2,1)} copy-done((bf16[2,2,512,256]{3,2,1,0:T(8,128)(2,1)}, bf16[2,2,512,256]{3,2,1,0:T(8,128)(2,1)S(1)}, u32[]{:S(2)}) %copy-start.6) | copy-done | bytes 1048600
  50.6 0.9 %copy-done.7 = bf16[8,32,1280]{2,1,0:T(8,128)(2,1)} copy-done((bf16[8,32,1280]{2,1,0:T(8,128)(2,1)}, bf16[8,32,1280]{2,1,0:T(8,128)(2,1)S(1)}, u32[]{:S(2)}) %copy-start.7) | copy-done | bytes 655384
  51.4 5.6 %coefficients.1 = (bf16[2,2,16,512]{3,2,1,0:T(8,128)(2,1)}, bf16[2,2,16,512]{3,2,1,0:T(8,128)(2,1)}) custom-call(s32[2]{0:T(128)} %pad_add_fusion.2.place_ref, s32[2,2,41]{2,1,0:T(2,128)} %pad_add_fusion.offsets_ref, s32[2,2]{1,0:T(2,128)} %fusion.8.totals_ref, bf16[8,32,1280]{2,1,0:T(8,128)(2,1)} %copy-done, bf16[8,32,1280]{2,1,0:T(8,128)(2,1)} %copy-done.7, ...), custom_call_target="tpu_custom_call" | custom-call | flops 2684354560 | bytes 4194304 | tf_op jit(solution)/shard_map/coefficients/pallas_call | solution.py:211
  57.0 1.5 %collective-permute-start.3 = (bf16[2,2,16,512]{3,2,1,0:T(8,128)(2,1)}, bf16[2,2,16,512]{3,2,1,0:T(8,128)(2,1)S(1)}, u32[]{:S(2)}, u32[]{:S(2)}) collective-permute-start(bf16[2,2,16,512]{3,2,1,0:T(8,128)(2,1)} %get-tuple-element.8), channel_id=1, source_target_pairs={{0,2},{1,3},{2,0},{3,1},{4,6},{5,7},{6,4},{7,5},{8,10},{9,11},{10,... | collective-permute-start | bytes 196616 | tf_op jit(solution)/shard_map/ppermute | solution.py:366
  58.5 3.0 %collective-permute-done.3.far_ref = bf16[2,2,16,512]{3,2,1,0:T(8,128)(2,1)S(1)} collective-permute-done((bf16[2,2,16,512]{3,2,1,0:T(8,128)(2,1)}, bf16[2,2,16,512]{3,2,1,0:T(8,128)(2,1)S(1)}, u32[]{:S(2)}, u32[]{:S(2)}) %collective-permute-start.3) | collective-permute-done | bytes 65568 | tf_op jit(solution)/shard_map/ppermute | solution.py:366
  61.5 0.6 copy-done.2
  62.1 2.5 %bands.1 = bf16[8,32,128]{2,1,0:T(8,128)(2,1)} custom-call(s32[2]{0:T(128)} %pad_add_fusion.2.place_ref, bf16[2,2,16,512]{3,2,1,0:T(8,128)(2,1)} %get-tuple-element.7.near_ref, bf16[2,2,16,512]{3,2,1,0:T(8,128)(2,1)} %copy-done.2, bf16[2,2,256,512]{3,2,1,0:T(8,128)(2,1)} %bitcast.14), custom_call_target="tpu_custom_call" | custom-call | flops 134217728 | bytes 2097152 | tf_op jit(solution)/shard_map/bands/pallas_call | solution.py:271
  64.6 5.7 %all-to-all-start.1 = ((bf16[8,32,128]{2,1,0:T(8,128)(2,1)}), bf16[8,32,128]{2,1,0:T(8,128)(2,1)S(1)}, u32[]{:S(2)}, u32[]{:S(2)}) async-start(bf16[8,32,128]{2,1,0:T(8,128)(2,1)} %bands.1), calls=%async_computation.1 | async-start | bytes 131072 | tf_op jit(solution)/shard_map/all_to_all | solution.py:368
  70.3 0.1 copy.13
  70.4 0.6 convert_element_type.36.inverse_ref
  71.0 6.2 %all-to-all-done.1.bands_ref = bf16[8,32,128]{2,1,0:T(8,128)(2,1)S(1)} async-done(((bf16[8,32,128]{2,1,0:T(8,128)(2,1)}), bf16[8,32,128]{2,1,0:T(8,128)(2,1)S(1)}, u32[]{:S(2)}, u32[]{:S(2)}) %all-to-all-start.1) | async-done | bytes 65568 | tf_op jit(solution)/shard_map/all_to_all | solution.py:368
  77.2 0.6 copy-done.1
  77.8 5.1 %series.1 = bf16[1024,1024]{1,0:T(8,128)(2,1)} custom-call(bf16[8,32,128]{2,1,0:T(8,128)(2,1)} %copy-done.1, bf16[32,1024]{1,0:T(8,128)(2,1)} %convert_element_type.36.inverse_ref), custom_call_target="tpu_custom_call" | custom-call | flops 67108864 | bytes 2097152 | tf_op jit(solution)/shard_map/series/pallas_call | solution.py:308
  (16 shorter events, 0.1 us)
Async XLA Ops:
  0.0 23.5 %copy-start.5 = (bf16[2,2,1,512,256]{4,3,2,1,0:T(8,128)(2,1)S(1)}, bf16[2,2,1,512,256]{4,3,2,1,0:T(8,128)(2,1)}, u32[]{:S(2)}) copy-start(bf16[2,2,1,512,256]{4,3,2,1,0:T(8,128)(2,1)} %param.7) | copy-start | bytes 3145732
  0.0 25.0 %copy-start.4 = (s32[2,1,40]{2,1,0:T(1,128)S(1)}, s32[2,1,40]{2,1,0:T(1,128)}, u32[]{:S(2)}) copy-start(s32[2,1,40]{2,1,0:T(1,128)} %param.8) | copy-start | bytes 964
  0.0 40.7 %copy-start.3 = (s32[2,1,40]{2,1,0:T(1,128)S(1)}, s32[2,1,40]{2,1,0:T(1,128)}, u32[]{:S(2)}) copy-start(s32[2,1,40]{2,1,0:T(1,128)} %param.9) | copy-start | bytes 964
  16.1 24.6 %all-to-all-start = ((bf16[8,32,1280]{2,1,0:T(8,128)(2,1)}), bf16[8,32,1280]{2,1,0:T(8,128)(2,1)S(1)}, u32[]{:S(2)}, u32[]{:S(2)}) async-start(bf16[8,32,1280]{2,1,0:T(8,128)(2,1)} %transform.1), calls=%async_computation | async-start | bytes 1310720 | tf_op jit(solution)/shard_map/all_to_all | solution.py:363
  23.5 26.1 %collective-permute-start.2 = (bf16[2,2,512,256]{3,2,1,0:T(8,128)(2,1)S(1)}, bf16[2,2,512,256]{3,2,1,0:T(8,128)(2,1)S(1)}, u32[]{:S(2)}, u32[]{:S(2)}) collective-permute-start(bf16[2,2,512,256]{3,2,1,0:T(8,128)(2,1)S(1)} %bitcast.22), channel_id=1, source_target_pairs={{0,2},{1,3},{2,0},{3,1},{4,6},{5,7},{6,4},{7,5},{8,10},{9,11},{10,... | collective-permute-start | bytes 3145736 | tf_op jit(solution)/shard_map/ppermute | solution.py:356
  40.7 8.9 %copy-start = (bf16[8,32,1280]{2,1,0:T(8,128)(2,1)}, bf16[8,32,1280]{2,1,0:T(8,128)(2,1)S(1)}, u32[]{:S(2)}) copy-start(bf16[8,32,1280]{2,1,0:T(8,128)(2,1)S(1)} %all-to-all-done.own_ref) | copy-start | bytes 1966084
  40.7 8.9 %collective-permute-start.1 = (bf16[8,32,1280]{2,1,0:T(8,128)(2,1)S(1)}, bf16[8,32,1280]{2,1,0:T(8,128)(2,1)S(1)}, u32[]{:S(2)}, u32[]{:S(2)}) collective-permute-start(bf16[8,32,1280]{2,1,0:T(8,128)(2,1)S(1)} %all-to-all-done.own_ref), channel_id=1, source_target_pairs={{0,1},{1,0},{2,3},{3,2},{4,5},{5,4},{6,7},{7,6},{8,9},{9,8},{10,11... | collective-permute-start | bytes 1966088 | tf_op jit(solution)/shard_map/ppermute | solution.py:364
  40.9 7.3 %collective-permute-start = (s32[2,41]{1,0:T(2,128)S(1)}, s32[2,41]{1,0:T(2,128)S(1)}, u32[]{:S(2)}, u32[]{:S(2)}) collective-permute-start(s32[2,41]{1,0:T(2,128)S(1)} %pad_add_fusion.1), channel_id=1, source_target_pairs={{0,2},{1,3},{2,0},{3,1},{4,6},{5,7},{6,4},{7,5},{8,10},{9,11},{10,... | collective-permute-start | bytes 992 | tf_op jit(solution)/shard_map/ppermute | solution.py:360
  49.6 1.0 %copy-start.6 = (bf16[2,2,512,256]{3,2,1,0:T(8,128)(2,1)}, bf16[2,2,512,256]{3,2,1,0:T(8,128)(2,1)S(1)}, u32[]{:S(2)}) copy-start(bf16[2,2,512,256]{3,2,1,0:T(8,128)(2,1)S(1)} %collective-permute-done.2.v_far_ref) | copy-start | bytes 3145732
  50.6 0.9 %copy-start.7 = (bf16[8,32,1280]{2,1,0:T(8,128)(2,1)}, bf16[8,32,1280]{2,1,0:T(8,128)(2,1)S(1)}, u32[]{:S(2)}) copy-start(bf16[8,32,1280]{2,1,0:T(8,128)(2,1)S(1)} %collective-permute-done.1.twin_ref) | copy-start | bytes 1966084
  57.0 4.5 %collective-permute-start.3 = (bf16[2,2,16,512]{3,2,1,0:T(8,128)(2,1)}, bf16[2,2,16,512]{3,2,1,0:T(8,128)(2,1)S(1)}, u32[]{:S(2)}, u32[]{:S(2)}) collective-permute-start(bf16[2,2,16,512]{3,2,1,0:T(8,128)(2,1)} %get-tuple-element.8), channel_id=1, source_target_pairs={{0,2},{1,3},{2,0},{3,1},{4,6},{5,7},{6,4},{7,5},{8,10},{9,11},{10,... | collective-permute-start | bytes 196616 | tf_op jit(solution)/shard_map/ppermute | solution.py:366
  61.5 0.6 copy-start.2
  64.6 12.6 %all-to-all-start.1 = ((bf16[8,32,128]{2,1,0:T(8,128)(2,1)}), bf16[8,32,128]{2,1,0:T(8,128)(2,1)S(1)}, u32[]{:S(2)}, u32[]{:S(2)}) async-start(bf16[8,32,128]{2,1,0:T(8,128)(2,1)} %bands.1), calls=%async_computation.1 | async-start | bytes 131072 | tf_op jit(solution)/shard_map/all_to_all | solution.py:368
  77.2 0.6 copy-start.1
